TPU v7x, 256 devices: a 4x2x16 block of a 4x16x16 slice. The times are simulated.
256 devices in a mesh: groups: 2 (over y), fsdp: 32 (over z, core), expert: 4 (over x).
Axes of the slice: x: 4, y: 2, z: 16, core: 2. Of those that a mesh axis runs over, the one named last changes fastest.
The devices are a block of a 4x16x16 slice.
Arguments:
- queries: bfloat16 [4096, 2048], P(('groups', 'fsdp'), 'expert'), parts along dimension 0, may hold values from -14 to 14
- keys: bfloat16 [64, 2048, 512], P(('groups', 'fsdp'), None, 'expert'), parts along dimension 0, may hold values from -14 to 14
- values: bfloat16 [64, 2048, 512], P(('groups', 'fsdp'), None, 'expert'), parts along dimension 0, may hold values from -4 to 4
- out_weight: bfloat16 [2048, 4096], P('expert', 'fsdp'), may hold values from -0.5 to 0.5
- residual: bfloat16 [4096, 4096], P(('groups', 'fsdp')), parts along dimension 0, may hold values from -3 to 3
- norm_gain: float32 [4096], replicated, may hold values from 0.5 to 1.5
- route_ids: int32 [4096, 2], P(('groups', 'fsdp')), parts along dimension 0, may hold values from 0 to 7, as said below
- route_slots: int32 [4096, 2], P(('groups', 'fsdp')), parts along dimension 0, may hold values from 0 to 23, as said below
- route_weights: int32 [4096, 2], P(('groups', 'fsdp')), parts along dimension 0, may hold values from 1 to 65535, as said below
- w_gate: bfloat16 [8, 4096, 7168], P('expert', None, 'fsdp'), may hold values from -0.09375 to 0.09375
- w_up: bfloat16 [8, 4096, 7168], P('expert', None, 'fsdp'), may hold values from -0.09375 to 0.09375
- w_down: bfloat16 [8, 7168, 4096], P('expert', 'fsdp'), may hold values from -0.0625 to 0.0625
Outputs:
- layer_out: bfloat16 [4096, 4096], P(('groups', 'fsdp'), 'expert'), parts along dimension 0
There are 2 independent parts, one for each index of `groups`. A program takes and returns all parts, laid end to end along the dimension named above; an argument that names none is the same for every part. Nothing has to cross between parts.
Inputs may be any that keep to these rules, and one draw needn't show every extreme that they name: `route_ids`: each row names two different experts. Among the rows of one block, no expert is named more than 24 times and no group of experts 2 g and 2 g + 1 more than 36 times; one expert, the same for all blocks, is named exactly 24 times in every block and its group exactly 36 times; every expert is named in every block. `route_slots`: within one block, the routes to one expert hold the slots 0 to their count - 1, each once. `route_weights`: the two entries of a row sum to 65536.
All inputs are finite; a program needn't handle non-finite values.
Results may differ from a plain program's by a relative error of at most 0.02.
Values may be sent and summed in bfloat16 or wider, within the bound.
A program may use at most 128 MiB of HBM per device.

v0:
```python
import jax
import jax.numpy as jnp
from jax import lax
from jax.sharding import PartitionSpec as P

HEAD_DIM = 128
GCAP = 36
eps = 1e-05


def copy_for_each(shard, axis):
    copies = jnp.broadcast_to(shard, (lax.axis_size(axis), *shard.shape))
    return lax.all_to_all(copies, axis, split_axis=0, concat_axis=0, tiled=True)


def taken_together(shard, axis):
    everything = copy_for_each(shard, axis)
    return jnp.sum(everything.astype(jnp.float32), axis=0)


def sent_together(arrays, axis, dim, along):
    columns = [a.reshape(*a.shape[:along], -1) for a in arrays]
    both = jnp.concatenate(columns, axis=along)
    result, at, outs = (lax.all_gather(both, axis, axis=dim, tiled=True), 0, [])
    for a, column in zip(arrays, columns):
        slab = result[..., at : at + column.shape[along]]
        outs.append(slab.reshape(*slab.shape[:along], *a.shape[along:]))
        at += column.shape[along]
    return tuple(outs)


def in_blocks(shard, dim, peers):
    before, after = (shard.shape[:dim], shard.shape[dim + 1 :])
    return jnp.moveaxis(shard.reshape(*before, peers, -1, *after), dim, 0)


def summed_on_arrival(shard, axis, dim):
    peers = lax.axis_size(axis)
    pieces = lax.all_to_all(in_blocks(shard, dim, peers), axis, 0, 0, tiled=True)
    return jnp.sum(pieces.astype(jnp.float32), axis=0)


def attend(queries, keys, values):
    block = queries.shape[0]
    context = keys.shape[1]
    kv_dev = keys.shape[2] // HEAD_DIM
    heads_dev = queries.shape[1] // HEAD_DIM
    group = heads_dev // kv_dev
    query_heads = queries.reshape(block, kv_dev, group, HEAD_DIM)
    key_heads = keys[0].reshape(context, kv_dev, HEAD_DIM)
    value_heads = values[0].reshape(context, kv_dev, HEAD_DIM)
    scores = jnp.einsum(
        "qcgd,kcd->cgqk", query_heads, key_heads, preferred_element_type=jnp.float32
    ) * HEAD_DIM ** (-0.5)
    key_pos = jnp.arange(context)
    query_pos = context - block + jnp.arange(block)
    allowed = key_pos[None, :] <= query_pos[:, None]
    masked = jnp.where(allowed, scores, -1e30)
    highest = jnp.max(masked, axis=-1, keepdims=True)
    weights = jnp.where(allowed, jnp.exp(masked - highest), 0.0)
    probs = (weights / jnp.sum(weights, axis=-1, keepdims=True)).astype(jnp.bfloat16)
    heads_out = jnp.einsum("cgqk,kcd->qcgd", probs, value_heads, preferred_element_type=jnp.float32)
    return heads_out.astype(jnp.bfloat16).reshape(block, heads_dev * HEAD_DIM)


def per_device(
    queries,
    keys,
    values,
    out_weight,
    residual,
    norm_gain,
    route_ids,
    route_slots,
    route_weights,
    w_gate,
    w_up,
    w_down,
):
    heads_out = attend(queries, keys, values)
    partial_attn = jnp.dot(
        heads_out,
        lax.all_gather(out_weight, "fsdp", axis=1, tiled=True),
        preferred_element_type=jnp.float32,
    )
    attn = taken_together(partial_attn.astype(jnp.bfloat16), "expert").astype(jnp.float32)
    hstate = (residual.astype(jnp.float32) + attn).astype(jnp.bfloat16)
    state = hstate.astype(jnp.float32)
    scale = lax.rsqrt(jnp.mean(state * state, axis=-1, keepdims=True) + eps)
    normed = (state * scale * norm_gain).astype(jnp.bfloat16)
    group_index = lax.axis_index("expert")
    first_expert = 2 * group_index
    within = route_ids - first_expert
    in_group = (within >= 0) & (within < 2)
    lead_count = jnp.sum((route_ids == first_expert).astype(jnp.int32))
    target = jnp.where(in_group, route_slots + within * lead_count, -1)
    row_ids = jnp.arange(GCAP)
    one_hot = (
        (target[None, :, 0] == row_ids[:, None]) | (target[None, :, 1] == row_ids[:, None])
    ).astype(jnp.bfloat16)
    dispatch = jnp.dot(one_hot, normed, preferred_element_type=jnp.float32).astype(jnp.bfloat16)
    second = (row_ids >= lead_count).astype(jnp.bfloat16)
    rows, labels = sent_together((dispatch, second), "fsdp", 0, 1)
    gate = jnp.einsum("nd,edf->enf", rows, w_gate, preferred_element_type=jnp.float32)
    upper = jnp.einsum("nd,edf->enf", rows, w_up, preferred_element_type=jnp.float32)
    labels_f = labels.astype(jnp.float32)
    keep = jnp.stack([1.0 - labels_f, labels_f], axis=0)[:, :, None]
    values_new = (jax.nn.silu(gate) * upper * keep).astype(jnp.bfloat16)
    flat_out = lax.psum_scatter(
        jnp.einsum("enf,efd->nd", values_new, w_down, preferred_element_type=jnp.float32).astype(
            jnp.bfloat16
        ),
        "fsdp",
        scatter_dimension=0,
        tiled=True,
    ).astype(jnp.float32)
    row_index = route_slots + within * lead_count
    safe_index = jnp.where(in_group, row_index, 0)
    shares = jnp.where(in_group, route_weights.astype(jnp.float32) / 65536.0, 0.0)
    picked = jnp.take(flat_out, safe_index, axis=0)
    contrib = jnp.sum(shares[:, :, None] * picked, axis=1)
    moe = summed_on_arrival(contrib.astype(jnp.bfloat16), "expert", 1)
    width = moe.shape[1]
    own_state = lax.dynamic_slice_in_dim(hstate, group_index * width, width, 1)
    return (own_state.astype(jnp.float32) + moe).astype(jnp.bfloat16)


def solution(mesh):
    in_specs = (
        P(("groups", "fsdp"), "expert"),
        P(("groups", "fsdp"), None, "expert"),
        P(("groups", "fsdp"), None, "expert"),
        P("expert", "fsdp"),
        P(("groups", "fsdp"), None),
        P(),
        P(("groups", "fsdp"), None),
        P(("groups", "fsdp"), None),
        P(("groups", "fsdp"), None),
        P("expert", None, "fsdp"),
        P("expert", None, "fsdp"),
        P("expert", "fsdp", None),
    )
    out_specs = P(("groups", "fsdp"), "expert")
    return jax.shard_map(
        per_device, mesh=mesh, in_specs=in_specs, out_specs=out_specs, check_vma=False
    )
```

profile of v0, /device:TPU:417, one launch (start us, length us, event | category | flops | bytes accessed | tf_op | source)
XLA Modules:
  0.0 382.8 jit_solution(10625348687652536732)
XLA Ops:
  6.6 0.7 all-gather.4.cloned.1.call-update
  7.3 0.1 iota_compare_fusion
  7.5 0.1 copy-done
  7.6 1.5 fusion.33
  9.1 0.5 fusion.7
  9.6 0.7 fusion.8
  10.4 0.1 copy.34
  10.4 86.3 %all-gather.4.cloned.1.call-done = bf16[512,4096]{1,0:T(8,128)(2,1)} async-done(((bf16[512,128]{1,0:T(8,128)(2,1)}), bf16[512,4096]{1,0:T(8,128)(2,1)}) %all-gather.4.cloned.1.call-update) | async-done | bytes 4194320 | tf_op jit(solution)/shard_map/all_gather | solution.py:83
  96.8 3.0 convolution_convert_fusion
  99.8 1.6 broadcast_in_dim.51
  101.4 4.1 %all-to-all-start = ((bf16[4,64,4096]{2,1,0:T(8,128)(2,1)}), bf16[4,64,4096]{2,1,0:T(8,128)(2,1)S(1)}, u32[]{:S(2)}, u32[]{:S(2)}) async-start(bf16[4,64,4096]{2,1,0:T(8,128)(2,1)} %broadcast_in_dim.51), calls=%async_computation | async-start | bytes 4194304 | tf_op jit(solution)/shard_map/all_to_all | solution.py:13
  105.6 0.6 fusion.30
  106.2 0.7 fusion.27
  106.9 0.7 broadcast_select_fusion
  107.6 23.8 %all-to-all-done = bf16[4,64,4096]{2,1,0:T(8,128)(2,1)S(1)} async-done(((bf16[4,64,4096]{2,1,0:T(8,128)(2,1)}), bf16[4,64,4096]{2,1,0:T(8,128)(2,1)S(1)}, u32[]{:S(2)}, u32[]{:S(2)}) %all-to-all-start) | async-done | bytes 2097184 | tf_op jit(solution)/shard_map/all_to_all | solution.py:13
  131.4 0.3 convert_reduce_fusion
  131.7 0.3 fusion.9
  132.0 0.3 convolution_convert_fusion.1
  132.4 0.8 maximum_bitcast_fusion
  133.2 76.2 %all-gather.6.cloned.1.call-done = bf16[32,36,4097]{2,1,0:T(8,128)(2,1)} async-done(((bf16[1,36,4097]{2,1,0:T(8,128)(2,1)}), bf16[32,36,4097]{2,1,0:T(8,128)(2,1)}) %all-gather.6.cloned.1.call-update) | async-done | bytes 9439504 | tf_op jit(solution)/shard_map/all_gather | solution.py:24
  209.4 14.2 %reshape.107 = bf16[1152,4097]{1,0:T(8,128)(2,1)} reshape(bf16[32,36,4097]{2,1,0:T(8,128)(2,1)} %all-gather.6.cloned.1.call-done) | data formatting | bytes 18878976
  223.6 1.1 convert_reduce_fusion.2
  224.8 9.8 %fusion.3 = f32[1152,448]{0,1:S(1)} fusion(bf16[4096,448]{0,1:T(8,128)(2,1)} %bitcast.70, bf16[1152,4097]{1,0:T(8,128)(2,1)} %reshape.107), kind=kOutput, calls=%fused_computation.4 | convolution fusion | flops 4227858432 | bytes 15171584
  234.6 4.9 %fusion.1 = f32[1152,448]{0,1:S(1)} fusion(bf16[4096,448]{0,1:T(8,128)(2,1)S(1)} %bitcast.71, bf16[1152,4097]{1,0:T(8,128)(2,1)S(1)} %copy-done.2), kind=kOutput, calls=%fused_computation.2 | convolution fusion | flops 4227858432 | bytes 15171584
  239.6 7.6 %bitcast_convert_fusion = bf16[1152,4096]{1,0:T(8,128)(2,1)} fusion(bf16[2,224,4096]{2,1,0:T(8,128)(2,1)S(1)} %copy-done.10, f32[2,1152,224]{1,2,0:T(8,128)S(1)} %bitcast.73, f32[2,1152,224]{1,2,0:T(8,128)S(1)} %bitcast.72, f32[2,1152]{1,0:T(2,128)S(1)} %pad_maximum_fusion), kind=kOutput, calls=%fused_computation.1 | convolution fusion | flops 4236189696 | bytes 17245184 | tf_op jit(solution)/shard_map/enf,efd->nd/dot_general | solution.py:110
  247.2 72.3 %fusion = bf16[40,4096]{1,0:T(8,128)(2,1)S(1)} fusion(bf16[1152,4096]{1,0:T(8,128)(2,1)} %bitcast_convert_fusion), kind=kCustom, calls=%all-reduce-scatter | all-reduce-scatter fusion | flops 5242881 | bytes 9765888
  319.6 5.8 %collective-permute-start = (bf16[40,4096]{1,0:T(8,128)(2,1)S(1)}, bf16[40,4096]{1,0:T(8,128)(2,1)S(1)}, u32[]{:S(2)}, u32[]{:S(2)}) collective-permute-start(bf16[40,4096]{1,0:T(8,128)(2,1)S(1)} %fusion), channel_id=1, source_target_pairs={{0,4},{4,8},{8,12},{12,16},{16,20},{20,24},{24,28},{28,32},{32,36}... | collective-permute-start | bytes 983048
  325.4 2.0 collective-permute-start.1
  327.4 2.0 collective-permute-start.2
  329.3 0.7 compare_and_fusion
  330.0 0.1 copy.37
  330.1 0.1 reshape.98
  330.3 5.3 %collective-permute-start.3 = (bf16[4,4096]{1,0:T(4,128)(2,1)S(1)}, bf16[4,4096]{1,0:T(4,128)(2,1)S(1)}, u32[]{:S(2)}, u32[]{:S(2)}) collective-permute-start(bf16[4,4096]{1,0:T(4,128)(2,1)S(1)} %slice.20), channel_id=1, source_target_pairs={{0,16},{4,20},{8,24},{12,28},{16,32},{20,36},{24,40},{28,44},{32,4... | collective-permute-start | bytes 98312
  335.6 0.1 copy.36
  335.7 0.1 copy.35
  335.8 0.6 dynamic-slice.4
  337.0 11.4 %collective-permute-done.3 = bf16[4,4096]{1,0:T(4,128)(2,1)S(1)} collective-permute-done((bf16[4,4096]{1,0:T(4,128)(2,1)S(1)}, bf16[4,4096]{1,0:T(4,128)(2,1)S(1)}, u32[]{:S(2)}, u32[]{:S(2)}) %collective-permute-start.3) | collective-permute-done | bytes 32800
  348.4 1.7 concatenate.4
  350.1 0.1 dynamic-slice_convert_fusion
  350.1 1.3 gather_fusion
  351.5 2.3 reshape.97
  353.8 5.3 %multiply_reduce_fusion = bf16[64,4096]{1,0:T(8,128)(2,1)S(1)} fusion(f32[64,2,4096]{2,1,0:T(2,128)} %reshape.97, pred[64,2]{1,0:T(8,128)(4,1)S(1)} %copy.36, f32[64,2]{1,0:T(8,128)S(1)} %copy.35), kind=kLoop, calls=%fused_computation.12 | loop fusion | flops 1310720 | bytes 2622080 | tf_op jit(solution)/shard_map/reduce_sum | solution.py:121
  359.0 0.4 convert_element_type.117
  359.4 0.9 copy.38
  360.4 4.0 %all-to-all-start.1 = ((bf16[4,64,1024]{2,1,0:T(8,128)(2,1)}), bf16[4,64,1024]{2,1,0:T(8,128)(2,1)S(1)}, u32[]{:S(2)}, u32[]{:S(2)}) async-start(bf16[4,64,1024]{2,1,0:T(8,128)(2,1)} %copy.38), calls=%async_computation.1 | async-start | bytes 1048576 | tf_op jit(solution)/shard_map/all_to_all | solution.py:39
  364.3 9.9 %all-to-all-done.1 = bf16[4,64,1024]{2,1,0:T(8,128)(2,1)S(1)} async-done(((bf16[4,64,1024]{2,1,0:T(8,128)(2,1)}), bf16[4,64,1024]{2,1,0:T(8,128)(2,1)S(1)}, u32[]{:S(2)}, u32[]{:S(2)}) %all-to-all-start.1) | async-done | bytes 524320 | tf_op jit(solution)/shard_map/all_to_all | solution.py:39
  374.2 0.1 convert_reduce_fusion.1
  374.3 1.6 add_convert_fusion.1
  (40 shorter events, 0.2 us)
Async XLA Ops:
  6.5 1.0 copy-start
  6.6 90.2 %all-gather.4.cloned.1.call-start = ((), (), s32[]{:S(2)}) async-start(), calls=%async_computation.2 | async-start | bytes 4325376 | tf_op jit(solution)/shard_map/all_gather | solution.py:83
  7.6 2.0 copy-start.11
  101.4 4.2 %copy-start.5 = (s32[64,2]{0,1:T(2,128)S(1)}, s32[64,2]{0,1:T(2,128)}, u32[]{:S(2)}) copy-start(s32[64,2]{0,1:T(2,128)} %param.18) | copy-start | bytes 1540
  101.4 5.5 %copy-start.7 = (s32[64,2]{0,1:T(2,128)S(1)}, s32[64,2]{0,1:T(2,128)}, u32[]{:S(2)}) copy-start(s32[64,2]{0,1:T(2,128)} %param.20) | copy-start | bytes 1540
  101.4 5.5 %copy-start.6 = (s32[64,2]{0,1:T(2,128)S(1)}, s32[64,2]{0,1:T(2,128)}, u32[]{:S(2)}) copy-start(s32[64,2]{0,1:T(2,128)} %param.19) | copy-start | bytes 1540
  101.4 30.0 %all-to-all-start = ((bf16[4,64,4096]{2,1,0:T(8,128)(2,1)}), bf16[4,64,4096]{2,1,0:T(8,128)(2,1)S(1)}, u32[]{:S(2)}, u32[]{:S(2)}) async-start(bf16[4,64,4096]{2,1,0:T(8,128)(2,1)} %broadcast_in_dim.51), calls=%async_computation | async-start | bytes 4194304 | tf_op jit(solution)/shard_map/all_to_all | solution.py:13
  105.5 26.2 %copy-start.4 = (bf16[64,4096]{1,0:T(8,128)(2,1)S(1)}, bf16[64,4096]{1,0:T(8,128)(2,1)}, u32[]{:S(2)}) copy-start(bf16[64,4096]{1,0:T(8,128)(2,1)} %param.16) | copy-start | bytes 1572868
  105.5 103.8 %all-gather.6.cloned.1.call-start = ((), (), s32[]{:S(2)}) async-start(), calls=%async_computation.3 | async-start | bytes 11151360 | tf_op jit(solution)/shard_map/all_gather | solution.py:24
  107.6 24.5 %copy-start.12 = (f32[4096]{0:T(1024)S(1)}, f32[4096]{0:T(1024)}, u32[]{:S(2)}) copy-start(f32[4096]{0:T(1024)} %param.17) | copy-start | bytes 49156
  132.0 91.6 %copy-start.3 = (bf16[64,4096]{1,0:T(8,128)(2,1)}, bf16[64,4096]{1,0:T(8,128)(2,1)S(1)}, u32[]{:S(2)}) copy-start(bf16[64,4096]{1,0:T(8,128)(2,1)S(1)} %get-tuple-element.10) | copy-start | bytes 1572868
  224.7 9.8 %copy-start.2 = (bf16[1152,4097]{1,0:T(8,128)(2,1)S(1)}, bf16[1152,4097]{1,0:T(8,128)(2,1)}, u32[]{:S(2)}) copy-start(bf16[1152,4097]{1,0:T(8,128)(2,1)} %reshape.107) | copy-start | bytes 28318468
  224.8 9.8 %copy-start.9 = (bf16[2,4096,224]{1,2,0:T(8,128)(2,1)S(1)}, bf16[2,4096,224]{1,2,0:T(8,128)(2,1)}, u32[]{:S(2)}) copy-start(bf16[2,4096,224]{1,2,0:T(8,128)(2,1)} %param.22) | copy-start | bytes 11010052
  234.6 5.0 %copy-start.10 = (bf16[2,224,4096]{2,1,0:T(8,128)(2,1)S(1)}, bf16[2,224,4096]{2,1,0:T(8,128)(2,1)}, u32[]{:S(2)}) copy-start(bf16[2,224,4096]{2,1,0:T(8,128)(2,1)} %param.23) | copy-start | bytes 11010052
  247.2 88.6 %copy-start.8 = (u32[256]{0:T(256)S(1)}, u32[256]{0:T(256)}, u32[]{:S(2)}) copy-start(u32[256]{0:T(256)} %constant.60) | copy-start | bytes 3076
  319.6 28.8 %collective-permute-start = (bf16[40,4096]{1,0:T(8,128)(2,1)S(1)}, bf16[40,4096]{1,0:T(8,128)(2,1)S(1)}, u32[]{:S(2)}, u32[]{:S(2)}) collective-permute-start(bf16[40,4096]{1,0:T(8,128)(2,1)S(1)} %fusion), channel_id=1, source_target_pairs={{0,4},{4,8},{8,12},{12,16},{16,20},{20,24},{24,28},{28,32},{32,36}... | collective-permute-start | bytes 983048
  325.4 23.0 %collective-permute-start.1 = (bf16[40,4096]{1,0:T(8,128)(2,1)S(1)}, bf16[40,4096]{1,0:T(8,128)(2,1)S(1)}, u32[]{:S(2)}, u32[]{:S(2)}) collective-permute-start(bf16[40,4096]{1,0:T(8,128)(2,1)S(1)} %fusion), channel_id=1, source_target_pairs={{0,8},{4,12},{8,16},{12,20},{16,24},{20,28},{24,32},{28,36},{32,40... | collective-permute-start | bytes 983048
  327.4 21.0 %collective-permute-start.2 = (bf16[40,4096]{1,0:T(8,128)(2,1)S(1)}, bf16[40,4096]{1,0:T(8,128)(2,1)S(1)}, u32[]{:S(2)}, u32[]{:S(2)}) collective-permute-start(bf16[40,4096]{1,0:T(8,128)(2,1)S(1)} %fusion), channel_id=1, source_target_pairs={{0,12},{4,16},{8,20},{12,24},{16,28},{20,32},{24,36},{28,40},{32,4... | collective-permute-start | bytes 983048
  330.3 18.1 %collective-permute-start.3 = (bf16[4,4096]{1,0:T(4,128)(2,1)S(1)}, bf16[4,4096]{1,0:T(4,128)(2,1)S(1)}, u32[]{:S(2)}, u32[]{:S(2)}) collective-permute-start(bf16[4,4096]{1,0:T(4,128)(2,1)S(1)} %slice.20), channel_id=1, source_target_pairs={{0,16},{4,20},{8,24},{12,28},{16,32},{20,36},{24,40},{28,44},{32,4... | collective-permute-start | bytes 98312
  353.8 22.1 %copy-start.1 = (bf16[1,2048,128]{2,1,0:T(8,128)(2,1)S(1)}, bf16[1,2048,128]{2,1,0:T(8,128)(2,1)}, u32[]{:S(2)}) copy-start(bf16[1,2048,128]{2,1,0:T(8,128)(2,1)} %param.13) | copy-start | bytes 1572868
  360.4 13.9 %all-to-all-start.1 = ((bf16[4,64,1024]{2,1,0:T(8,128)(2,1)}), bf16[4,64,1024]{2,1,0:T(8,128)(2,1)S(1)}, u32[]{:S(2)}, u32[]{:S(2)}) async-start(bf16[4,64,1024]{2,1,0:T(8,128)(2,1)} %copy.38), calls=%async_computation.1 | async-start | bytes 1048576 | tf_op jit(solution)/shard_map/all_to_all | solution.py:39
Sparse Core Ops, SparseCore 0:
  9.1 87.5 all-gather.3
  133.3 76.0 all-gather.5
where the time goes:
time: 384 us; the launch traced here: 383 us
  waiting for transfers between devices  208 us (54%)
  blocking collectives  72.3 us (19%)
  matrix products  27.9 us (7%)
  local copies, waits for them, and re-layouts  23.7 us (6%)
  starting transfers between devices  23.1 us (6%)
  between operations  14.4 us (4%)
  other arithmetic  12.8 us (3%)
    all_gather x1, waiting for transfers between devices, per_device(): lax.all_gather(out_weight, 'fsdp', axis=1, tiled=True)  86.3 us
    all_gather x1, waiting for transfers between devices, sent_together(): result, at, outs = (lax.all_gather(both, axis, axis=dim, tiled=True), 0, [])  76.2 us
    unnamed x1, blocking collectives  72.3 us
    all_to_all x1, waiting for transfers between devices, copy_for_each(): return lax.all_to_all(copies, axis, split_axis=0, concat_axis=0, tiled=True)  23.8 us
    unnamed x30, local copies, waits for them, and re-layouts  16.7 us
    unnamed x4, starting transfers between devices  15 us
    unnamed x2, matrix products  14.7 us
    unnamed x6, waiting for transfers between devices  12.2 us
  transfers between devices with their start and end apart: 8, of which 5 were waited for; matrix products, arithmetic and copies ran while one was open for 2% of the time, Pallas kernels for 0%

commit v1 on v0

--- a/solution.py
+++ b/solution.py
@@ -6,6 +6,12 @@
 HEAD_DIM = 128
 GCAP = 36
 eps = 1e-05
+
+
+def gather_by_exchange(x, axis, dim):
+    count = lax.axis_size(axis)
+    repeats = [count if d == dim else 1 for d in range(x.ndim)]
+    return lax.all_to_all(jnp.tile(x, repeats), axis, split_axis=dim, concat_axis=dim, tiled=True)
 
 
 def copy_for_each(shard, axis):
@@ -79,9 +85,7 @@
 ):
     heads_out = attend(queries, keys, values)
     partial_attn = jnp.dot(
-        heads_out,
-        lax.all_gather(out_weight, "fsdp", axis=1, tiled=True),
-        preferred_element_type=jnp.float32,
+        heads_out, gather_by_exchange(out_weight, "fsdp", 1), preferred_element_type=jnp.float32
     )
     attn = taken_together(partial_attn.astype(jnp.bfloat16), "expert").astype(jnp.float32)
     hstate = (residual.astype(jnp.float32) + attn).astype(jnp.bfloat16)

time: 384 us -> 511 us (1.33)
  waiting for transfers between devices: 208 us -> 304 us
  starting transfers between devices: 23.1 us -> 44.5 us
  local copies, waits for them, and re-layouts: 23.7 us -> 34 us
    all_to_all x0 -> x1, waiting for transfers between devices: none -> 182 us  [gather_by_exchange(): lax.all_to_all(jnp.tile(x, repeats), axis, split_axis=dim, concat_axis=di...]
    all_gather x1 -> x0, waiting for transfers between devices: 86.3 us -> none  [per_device(): lax.all_gather(out_weight, 'fsdp', axis=1, tiled=True)]
    all_to_all x0 -> x1, starting transfers between devices: none -> 21 us  [gather_by_exchange(): lax.all_to_all(jnp.tile(x, repeats), axis, split_axis=dim, concat_axis=di...]
    all_to_all x0 -> x1, local copies, waits for them, and re-layouts: none -> 6.51 us  [gather_by_exchange(): lax.all_to_all(jnp.tile(x, repeats), axis, split_axis=dim, concat_axis=di...]
    unnamed x6 -> x5, waiting for transfers between devices: 12.2 us -> 11.4 us
    unnamed x30 -> x32, local copies, waits for them, and re-layouts: 16.7 us -> 16.5 us
  transfers between devices with their start and end apart: 8 -> 8, of which waited for: 5 -> 5; matrix products, arithmetic and copies ran while one was open for 2% -> 1% of each run, Pallas kernels for 0% -> 0%
where the time goes in v1:
time: 511 us; the launch traced here: 510 us
  waiting for transfers between devices  304 us (59%)
  blocking collectives  72.3 us (14%)
  starting transfers between devices  44.5 us (9%)
  local copies, waits for them, and re-layouts  34 us (7%)
  matrix products  27.6 us (5%)
  between operations  14.4 us (3%)
  other arithmetic  12.8 us (3%)
    all_to_all x1, waiting for transfers between devices, gather_by_exchange(): lax.all_to_all(jnp.tile(x, repeats), axis, split_axis=dim, concat_axis=di...  182 us
    all_gather x1, waiting for transfers between devices, sent_together(): result, at, outs = (lax.all_gather(both, axis, axis=dim, tiled=True), 0, [])  78.2 us
    unnamed x1, blocking collectives  72.3 us
    all_to_all x1, waiting for transfers between devices, copy_for_each(): return lax.all_to_all(copies, axis, split_axis=0, concat_axis=0, tiled=True)  22.7 us
    all_to_all x1, starting transfers between devices, gather_by_exchange(): lax.all_to_all(jnp.tile(x, repeats), axis, split_axis=dim, concat_axis=di...  21 us
    unnamed x32, local copies, waits for them, and re-layouts  16.5 us
    unnamed x4, starting transfers between devices  15 us
    unnamed x2, matrix products  14.7 us
  transfers between devices with their start and end apart: 8, of which 5 were waited for; matrix products, arithmetic and copies ran while one was open for 1% of the time, Pallas kernels for 0%

profile of v1, /device:TPU:417, one launch (start us, length us, event | category | flops | bytes accessed | tf_op | source)
XLA Modules:
  0.0 510.0 jit_solution(15715607884456569641)
XLA Ops:
  6.6 3.9 tile.2
  10.4 21.0 %all-to-all-start = ((bf16[512,32,128]{2,0,1:T(8,128)(2,1)}), bf16[512,32,128]{2,0,1:T(8,128)(2,1)}, u32[]{:S(2)}, u32[]{:S(2)}) async-start(bf16[512,32,128]{2,0,1:T(8,128)(2,1)} %tile.2), calls=%async_computation | async-start | bytes 8388608 | tf_op jit(solution)/shard_map/all_to_all | solution.py:14
  31.5 0.1 iota_compare_fusion
  31.7 0.6 fusion.33
  32.2 0.5 fusion.7
  32.8 0.7 fusion.8
  33.6 182.1 %all-to-all-done = bf16[512,32,128]{2,0,1:T(8,128)(2,1)} async-done(((bf16[512,32,128]{2,0,1:T(8,128)(2,1)}), bf16[512,32,128]{2,0,1:T(8,128)(2,1)}, u32[]{:S(2)}, u32[]{:S(2)}) %all-to-all-start) | async-done | bytes 4194336 | tf_op jit(solution)/shard_map/all_to_all | solution.py:14
  215.7 6.5 %copy.36 = bf16[512,32,128]{0,2,1:T(8,128)(2,1)} copy(bf16[512,32,128]{2,0,1:T(8,128)(2,1)} %all-to-all-done) | data formatting | bytes 8388608 | tf_op jit(solution)/shard_map/all_to_all | solution.py:14
  222.2 3.6 convolution_convert_fusion
  225.8 1.6 broadcast_in_dim.51
  227.4 4.4 all-to-all-start.1
  231.8 0.6 fusion.30
  232.4 0.7 fusion.27
  233.1 0.7 broadcast_select_fusion
  233.8 22.7 %all-to-all-done.1 = bf16[4,64,4096]{2,1,0:T(8,128)(2,1)S(1)} async-done(((bf16[4,64,4096]{2,1,0:T(8,128)(2,1)}), bf16[4,64,4096]{2,1,0:T(8,128)(2,1)S(1)}, u32[]{:S(2)}, u32[]{:S(2)}) %all-to-all-start.1) | async-done | bytes 2097184 | tf_op jit(solution)/shard_map/all_to_all | solution.py:19
  256.6 0.3 convert_reduce_fusion
  256.9 0.3 fusion.9
  257.2 0.3 convolution_convert_fusion.1
  257.5 0.8 maximum_bitcast_fusion
  258.4 78.2 %all-gather.3.cloned.1.call-done = bf16[32,36,4097]{2,1,0:T(8,128)(2,1)} async-done(((bf16[1,36,4097]{2,1,0:T(8,128)(2,1)}), bf16[32,36,4097]{2,1,0:T(8,128)(2,1)}) %all-gather.3.cloned.1.call-update) | async-done | bytes 9439504 | tf_op jit(solution)/shard_map/all_gather | solution.py:30
  336.6 14.2 %reshape.114 = bf16[1152,4097]{1,0:T(8,128)(2,1)} reshape(bf16[32,36,4097]{2,1,0:T(8,128)(2,1)} %all-gather.3.cloned.1.call-done) | data formatting | bytes 18878976
  350.8 1.1 convert_reduce_fusion.2
  352.0 9.8 %fusion.3 = f32[1152,448]{0,1:S(1)} fusion(bf16[4096,448]{0,1:T(8,128)(2,1)} %bitcast.72, bf16[1152,4097]{1,0:T(8,128)(2,1)} %reshape.114), kind=kOutput, calls=%fused_computation.4 | convolution fusion | flops 4227858432 | bytes 15171584
  361.8 4.9 fusion.1
  366.8 7.6 %bitcast_convert_fusion = bf16[1152,4096]{1,0:T(8,128)(2,1)} fusion(bf16[2,224,4096]{2,1,0:T(8,128)(2,1)S(1)} %copy-done.11, f32[2,1152,224]{1,2,0:T(8,128)S(1)} %bitcast.75, f32[2,1152,224]{1,2,0:T(8,128)S(1)} %bitcast.74, f32[2,1152]{1,0:T(2,128)S(1)} %pad_maximum_fusion), kind=kOutput, calls=%fused_computation.1 | convolution fusion | flops 4236189696 | bytes 17245184 | tf_op jit(solution)/shard_map/enf,efd->nd/dot_general | solution.py:114
  374.5 72.3 %fusion = bf16[40,4096]{1,0:T(8,128)(2,1)S(1)} fusion(bf16[1152,4096]{1,0:T(8,128)(2,1)} %bitcast_convert_fusion), kind=kCustom, calls=%all-reduce-scatter | all-reduce-scatter fusion | flops 5242881 | bytes 9765888
  446.8 5.8 %collective-permute-start = (bf16[40,4096]{1,0:T(8,128)(2,1)S(1)}, bf16[40,4096]{1,0:T(8,128)(2,1)S(1)}, u32[]{:S(2)}, u32[]{:S(2)}) collective-permute-start(bf16[40,4096]{1,0:T(8,128)(2,1)S(1)} %fusion), channel_id=1, source_target_pairs={{0,4},{4,8},{8,12},{12,16},{16,20},{20,24},{24,28},{28,32},{32,36}... | collective-permute-start | bytes 983048
  452.7 2.0 collective-permute-start.1
  454.6 2.0 collective-permute-start.2
  456.6 0.7 compare_and_fusion
  457.2 0.1 copy.39
  457.3 0.1 reshape.105
  457.5 5.3 %collective-permute-start.3 = (bf16[4,4096]{1,0:T(4,128)(2,1)S(1)}, bf16[4,4096]{1,0:T(4,128)(2,1)S(1)}, u32[]{:S(2)}, u32[]{:S(2)}) collective-permute-start(bf16[4,4096]{1,0:T(4,128)(2,1)S(1)} %slice.20), channel_id=1, source_target_pairs={{0,16},{4,20},{8,24},{12,28},{16,32},{20,36},{24,40},{28,44},{32,4... | collective-permute-start | bytes 98312
  462.8 0.1 copy.38
  462.9 0.1 copy.37
  463.0 0.6 dynamic-slice.4
  464.3 11.4 %collective-permute-done.3 = bf16[4,4096]{1,0:T(4,128)(2,1)S(1)} collective-permute-done((bf16[4,4096]{1,0:T(4,128)(2,1)S(1)}, bf16[4,4096]{1,0:T(4,128)(2,1)S(1)}, u32[]{:S(2)}, u32[]{:S(2)}) %collective-permute-start.3) | collective-permute-done | bytes 32800
  475.6 1.7 concatenate.4
  477.3 0.1 dynamic-slice_convert_fusion
  477.4 1.3 gather_fusion
  478.7 2.3 reshape.104
  481.0 5.3 %multiply_reduce_fusion = bf16[64,4096]{1,0:T(8,128)(2,1)S(1)} fusion(f32[64,2,4096]{2,1,0:T(2,128)} %reshape.104, pred[64,2]{1,0:T(8,128)(4,1)S(1)} %copy.38, f32[64,2]{1,0:T(8,128)S(1)} %copy.37), kind=kLoop, calls=%fused_computation.12 | loop fusion | flops 1310720 | bytes 2622080 | tf_op jit(solution)/shard_map/reduce_sum | solution.py:125
  486.3 0.4 convert_element_type.117
  486.7 0.9 copy.40
  487.6 4.0 all-to-all-start.2
  491.6 9.9 %all-to-all-done.2 = bf16[4,64,1024]{2,1,0:T(8,128)(2,1)S(1)} async-done(((bf16[4,64,1024]{2,1,0:T(8,128)(2,1)}), bf16[4,64,1024]{2,1,0:T(8,128)(2,1)S(1)}, u32[]{:S(2)}, u32[]{:S(2)}) %all-to-all-start.2) | async-done | bytes 524320 | tf_op jit(solution)/shard_map/all_to_all | solution.py:45
  501.5 0.1 convert_reduce_fusion.1
  501.6 1.6 add_convert_fusion.1
  (43 shorter events, 0.3 us)
Async XLA Ops:
  6.5 25.1 %copy-start = (bf16[1,2048,128]{2,1,0:T(8,128)(2,1)S(1)}, bf16[1,2048,128]{2,1,0:T(8,128)(2,1)}, u32[]{:S(2)}) copy-start(bf16[1,2048,128]{2,1,0:T(8,128)(2,1)} %param.13) | copy-start | bytes 1572868
  10.4 21.2 %copy-start.5 = (bf16[64,512]{1,0:T(8,128)(2,1)S(1)}, bf16[64,512]{1,0:T(8,128)(2,1)}, u32[]{:S(2)}) copy-start(bf16[64,512]{1,0:T(8,128)(2,1)} %param.12) | copy-start | bytes 196612
  10.4 205.2 %all-to-all-start = ((bf16[512,32,128]{2,0,1:T(8,128)(2,1)}), bf16[512,32,128]{2,0,1:T(8,128)(2,1)}, u32[]{:S(2)}, u32[]{:S(2)}) async-start(bf16[512,32,128]{2,0,1:T(8,128)(2,1)} %tile.2), calls=%async_computation | async-start | bytes 8388608 | tf_op jit(solution)/shard_map/all_to_all | solution.py:14
  31.6 1.1 copy-start.12
  227.4 4.4 copy-start.6
  227.4 5.7 %copy-start.8 = (s32[64,2]{0,1:T(2,128)S(1)}, s32[64,2]{0,1:T(2,128)}, u32[]{:S(2)}) copy-start(s32[64,2]{0,1:T(2,128)} %param.20) | copy-start | bytes 1540
  227.4 5.8 %copy-start.7 = (s32[64,2]{0,1:T(2,128)S(1)}, s32[64,2]{0,1:T(2,128)}, u32[]{:S(2)}) copy-start(s32[64,2]{0,1:T(2,128)} %param.19) | copy-start | bytes 1540
  227.4 29.2 %all-to-all-start.1 = ((bf16[4,64,4096]{2,1,0:T(8,128)(2,1)}), bf16[4,64,4096]{2,1,0:T(8,128)(2,1)S(1)}, u32[]{:S(2)}, u32[]{:S(2)}) async-start(bf16[4,64,4096]{2,1,0:T(8,128)(2,1)} %broadcast_in_dim.51), calls=%async_computation.1 | async-start | bytes 4194304 | tf_op jit(solution)/shard_map/all_to_all | solution.py:19
  231.8 25.1 %copy-start.4 = (bf16[64,4096]{1,0:T(8,128)(2,1)S(1)}, bf16[64,4096]{1,0:T(8,128)(2,1)}, u32[]{:S(2)}) copy-start(bf16[64,4096]{1,0:T(8,128)(2,1)} %param.16) | copy-start | bytes 1572868
  231.8 104.8 %all-gather.3.cloned.1.call-start = ((), (), s32[]{:S(2)}) async-start(), calls=%async_computation.3 | async-start | bytes 11151360 | tf_op jit(solution)/shard_map/all_gather | solution.py:30
  233.8 23.4 %copy-start.13 = (f32[4096]{0:T(1024)S(1)}, f32[4096]{0:T(1024)}, u32[]{:S(2)}) copy-start(f32[4096]{0:T(1024)} %param.17) | copy-start | bytes 49156
  257.2 93.7 %copy-start.3 = (bf16[64,4096]{1,0:T(8,128)(2,1)}, bf16[64,4096]{1,0:T(8,128)(2,1)S(1)}, u32[]{:S(2)}) copy-start(bf16[64,4096]{1,0:T(8,128)(2,1)S(1)} %get-tuple-element.10) | copy-start | bytes 1572868
  352.0 9.8 %copy-start.2 = (bf16[1152,4097]{1,0:T(8,128)(2,1)S(1)}, bf16[1152,4097]{1,0:T(8,128)(2,1)}, u32[]{:S(2)}) copy-start(bf16[1152,4097]{1,0:T(8,128)(2,1)} %reshape.114) | copy-start | bytes 28318468
  352.0 9.8 %copy-start.10 = (bf16[2,4096,224]{1,2,0:T(8,128)(2,1)S(1)}, bf16[2,4096,224]{1,2,0:T(8,128)(2,1)}, u32[]{:S(2)}) copy-start(bf16[2,4096,224]{1,2,0:T(8,128)(2,1)} %param.22) | copy-start | bytes 11010052
  361.8 5.0 copy-start.11
  374.4 88.6 %copy-start.9 = (u32[256]{0:T(256)S(1)}, u32[256]{0:T(256)}, u32[]{:S(2)}) copy-start(u32[256]{0:T(256)} %constant.60) | copy-start | bytes 3076
  446.8 28.8 %collective-permute-start = (bf16[40,4096]{1,0:T(8,128)(2,1)S(1)}, bf16[40,4096]{1,0:T(8,128)(2,1)S(1)}, u32[]{:S(2)}, u32[]{:S(2)}) collective-permute-start(bf16[40,4096]{1,0:T(8,128)(2,1)S(1)} %fusion), channel_id=1, source_target_pairs={{0,4},{4,8},{8,12},{12,16},{16,20},{20,24},{24,28},{28,32},{32,36}... | collective-permute-start | bytes 983048
  452.7 23.0 %collective-permute-start.1 = (bf16[40,4096]{1,0:T(8,128)(2,1)S(1)}, bf16[40,4096]{1,0:T(8,128)(2,1)S(1)}, u32[]{:S(2)}, u32[]{:S(2)}) collective-permute-start(bf16[40,4096]{1,0:T(8,128)(2,1)S(1)} %fusion), channel_id=1, source_target_pairs={{0,8},{4,12},{8,16},{12,20},{16,24},{20,28},{24,32},{28,36},{32,40... | collective-permute-start | bytes 983048
  454.6 21.0 %collective-permute-start.2 = (bf16[40,4096]{1,0:T(8,128)(2,1)S(1)}, bf16[40,4096]{1,0:T(8,128)(2,1)S(1)}, u32[]{:S(2)}, u32[]{:S(2)}) collective-permute-start(bf16[40,4096]{1,0:T(8,128)(2,1)S(1)} %fusion), channel_id=1, source_target_pairs={{0,12},{4,16},{8,20},{12,24},{16,28},{20,32},{24,36},{28,40},{32,4... | collective-permute-start | bytes 983048
  457.5 18.1 %collective-permute-start.3 = (bf16[4,4096]{1,0:T(4,128)(2,1)S(1)}, bf16[4,4096]{1,0:T(4,128)(2,1)S(1)}, u32[]{:S(2)}, u32[]{:S(2)}) collective-permute-start(bf16[4,4096]{1,0:T(4,128)(2,1)S(1)} %slice.20), channel_id=1, source_target_pairs={{0,16},{4,20},{8,24},{12,28},{16,32},{20,36},{24,40},{28,44},{32,4... | collective-permute-start | bytes 98312
  481.0 22.2 %copy-start.1 = (bf16[1,2048,128]{2,1,0:T(8,128)(2,1)S(1)}, bf16[1,2048,128]{2,1,0:T(8,128)(2,1)}, u32[]{:S(2)}) copy-start(bf16[1,2048,128]{2,1,0:T(8,128)(2,1)} %param.13) | copy-start | bytes 1572868
  487.6 13.9 %all-to-all-start.2 = ((bf16[4,64,1024]{2,1,0:T(8,128)(2,1)}), bf16[4,64,1024]{2,1,0:T(8,128)(2,1)S(1)}, u32[]{:S(2)}, u32[]{:S(2)}) async-start(bf16[4,64,1024]{2,1,0:T(8,128)(2,1)} %copy.40), calls=%async_computation.2 | async-start | bytes 1048576 | tf_op jit(solution)/shard_map/all_to_all | solution.py:45
Sparse Core Ops, SparseCore 0:
  258.5 78.0 all-gather.2
